TPU v7x, 32 devices: a whole 2x2x4 slice. The times are simulated.
32 devices in a mesh: au: 4 (over y, x), pa: 4 (over z), dev: 2 (over core).
Axes of the slice: x: 2, y: 2, z: 4, core: 2. Of those that a mesh axis runs over, the one named last changes fastest.
Arguments:
- features: bfloat16 [4096, 64, 256], P('au', 'pa'), may hold values from -6 to 6
- item_ids: int32 [4096, 64], P('au', 'pa'), may hold values from 0 to 4095
- item_table: bfloat16 [4096, 256], replicated, may hold values from -4 to 4
- lengths: int32 [4096], P('au'), may hold values from 1 to 64
- routing_seed: int32 [4, 64], replicated, may hold values from 0 to 15
- w_qkv: bfloat16 [3, 256, 256], P(None, None, 'dev'), may hold values from -0.375 to 0.375
- w_out: bfloat16 [256, 256], P('dev'), may hold values from -0.375 to 0.375
- w_bilinear: bfloat16 [256, 256], P(None, 'dev'), may hold values from -0.375 to 0.375
- w_up: bfloat16 [256, 1024], P(None, 'dev'), may hold values from -0.375 to 0.375
- w_down: bfloat16 [1024, 256], P('dev'), may hold values from -0.1875 to 0.1875
Outputs:
- capsules: float32 [4096, 4, 256], P(('au', 'pa'), None, 'dev')
All inputs are finite; a program needn't handle non-finite values.
Results may differ from a plain program's by a relative error of at most 0.012.
The roundings to bfloat16 on the way count: a program that leaves them out, or rounds other values in their place, can miss the bound.
Values may be sent and summed in bfloat16 or wider, within the bound.
A program may use at most 128 MiB of HBM per device.

v0:
```python
import functools

import jax
import jax.numpy as jnp
from jax import lax
from jax.experimental import pallas as pl
from jax.experimental.pallas import tpu as pltpu
from jax.sharding import PartitionSpec as P

D = 256
HEADS = 4
CAPS = 4
ITERS = 3


def local_routing(vectors, valid, base):
    user_count, history_len, width_here = vectors.shape
    logits = jnp.broadcast_to(base[None], (user_count, CAPS, history_len))
    capsules = jnp.zeros((user_count, CAPS, width_here), jnp.float32)
    for sweep in range(ITERS):
        weights = jax.nn.softmax(logits, axis=1) * valid[:, None, :]
        summed = jnp.einsum("ukl,uld->ukd", weights, vectors, precision=lax.Precision.HIGHEST)
        squares = jnp.sum(summed * summed, axis=-1)
        factor = jnp.sqrt(squares) / (1.0 + squares)
        capsules = summed * factor[..., None]
        if sweep + 1 < ITERS:
            logits = logits + jnp.einsum(
                "ukd,uld->ukl", capsules, vectors, precision=lax.Precision.HIGHEST
            )
    return capsules


def plain_body(
    features, item_ids, item_table, lengths, routing_seed, w_qkv, w_out, w_bilinear, w_up, w_down
):
    pa_count = lax.axis_size("pa")
    dev_count = lax.axis_size("dev")
    owned_users = lengths.shape[0] // pa_count
    head_size = D // HEADS
    share = owned_users // dev_count
    core = lax.axis_index("dev")

    def pick(array):
        shaped = array.reshape((pa_count, dev_count, share) + array.shape[1:])
        chosen = lax.dynamic_index_in_dim(shaped, core, 1, keepdims=False)
        return chosen.reshape((pa_count * share,) + array.shape[1:])

    features = pick(features)
    item_ids = pick(item_ids)
    lengths = pick(lengths)
    w_qkv, w_out, w_bilinear, w_up, w_down = (
        lax.all_gather(w_qkv, "dev", axis=2, tiled=True),
        lax.all_gather(w_out, "dev", axis=0, tiled=True),
        lax.all_gather(w_bilinear, "dev", axis=1, tiled=True),
        lax.all_gather(w_up, "dev", axis=1, tiled=True),
        lax.all_gather(w_down, "dev", axis=0, tiled=True),
    )
    own_lens = lax.dynamic_slice_in_dim(lengths, lax.axis_index("pa") * share, share)
    features, item_ids = (
        lax.all_to_all(features, "pa", split_axis=0, concat_axis=1, tiled=True),
        lax.all_to_all(item_ids, "pa", split_axis=0, concat_axis=1, tiled=True),
    )
    user_count, span_here, model_width = features.shape
    heads_here = w_qkv.shape[2] // head_size
    inputs = (
        features.astype(jnp.float32) + jnp.take(item_table, item_ids, axis=0).astype(jnp.float32)
    ).astype(jnp.bfloat16)
    flat_rows = inputs.reshape(-1, model_width)

    def project(index):
        shaped = w_qkv[index].reshape(model_width, heads_here, head_size)
        made = jnp.einsum(
            "nd,dhe->hne", flat_rows, shaped, preferred_element_type=jnp.float32
        ).astype(jnp.bfloat16)
        return made.reshape(heads_here, user_count, span_here, head_size)

    queries = project(0)
    key_block = project(1)
    value_block = project(2)
    score_scale = 1.0 / head_size**0.5
    count_here = key_block.shape[2]
    scores = (
        jnp.einsum("huqe,huke->huqk", queries, key_block, preferred_element_type=jnp.float32)
        * score_scale
    )
    positions = jnp.arange(count_here, dtype=jnp.int32)
    valid_keys = positions[None, :] < own_lens[:, None]
    mask_four = valid_keys[None, :, None, :]
    probs = jnp.where(mask_four, jnp.exp(scores), 0.0)
    totals = jnp.sum(probs, axis=-1)
    weighted = jnp.einsum(
        "huqk,huke->huqe",
        probs.astype(jnp.bfloat16),
        value_block,
        preferred_element_type=jnp.float32,
    )
    attended = (weighted / totals[..., None]).astype(jnp.bfloat16)
    out_heads = w_out.reshape(heads_here, head_size, w_out.shape[1])
    attended_term = jnp.einsum(
        "huqe,hef->uqf", attended, out_heads, preferred_element_type=jnp.float32
    )
    hidden = jax.nn.gelu(jnp.dot(flat_rows, w_up, preferred_element_type=jnp.float32)).astype(
        jnp.bfloat16
    )
    partial_terms = attended_term.reshape(-1, w_out.shape[1]) + jnp.dot(
        hidden, w_down, preferred_element_type=jnp.float32
    )
    interest_in = (
        partial_terms + jnp.dot(flat_rows, w_bilinear, preferred_element_type=jnp.float32)
    ).astype(jnp.bfloat16)
    interest_in = interest_in.reshape(user_count, span_here, -1)
    history_len = interest_in.shape[1]
    valid = (jnp.arange(history_len)[None, :] < own_lens[:, None]).astype(jnp.float32)
    base = (routing_seed.astype(jnp.float32) - 7.5) * 0.25
    routed = local_routing(interest_in.astype(jnp.float32), valid, base)
    capsules = lax.all_to_all(routed, "dev", split_axis=2, concat_axis=0, tiled=True)
    return capsules


GROUP = 8
F32, BF16 = jnp.float32, jnp.bfloat16
NT = (((1,), (1,)), ((), ()))


def dot(a, b):
    return jnp.dot(a, b, preferred_element_type=F32)


def split(a):
    high = a.astype(BF16)
    low = (a - high.astype(F32)).astype(BF16)
    return jnp.concatenate([high, low], axis=0)


def fused(
    n, share, chunk, ids, lens, feats, table, base, w_qkv, w_out, w_bil, w_up, w_down,
    out, stage, recv, table_in, table_wide, rows, w_in, w_mix, blocks, qkv, mix, high, low,
    weighted, interests, outbox, feat_sem, table_sem, own_sem, wsend_sem, wrecv_sem, send_sem, recv_sem,
    xsend_sem, xrecv_sem,
):
    me = lax.axis_index("pa")
    core = lax.axis_index("dev")
    sibling = 1 - core
    span, width = feats.shape[1], feats.shape[2]
    history = n * span
    head = width // HEADS
    half = width // 2
    chunks = share // chunk

    def owner(step):
        return lax.rem(me + step + 1, n)

    def first_user(step):
        return (owner(step) * 2 + core) * share

    table_copy = pltpu.make_async_copy(table, table_in, table_sem)
    table_copy.start()
    feat_copies = []
    for step in range(n):
        copy = pltpu.make_async_copy(
            feats.at[pl.ds(first_user(step), share)], stage.at[step], feat_sem.at[step]
        )
        copy.start()
        feat_copies.append(copy)

    up_half = w_up.shape[1]
    down_half = w_down.shape[0]

    def cols(start, size):
        return pl.ds(pl.multiple_of(start, 128), size)

    pieces = [
        (w_qkv.at[i], w_in.at[:, cols(i * width + core * half, half)]) for i in range(3)
    ] + [
        (w_up, w_in.at[:, cols(3 * width + core * up_half, up_half)]),
        (w_bil, w_mix.at[pl.ds(0, width), cols(core * half, half)]),
        (w_out, w_mix.at[cols(width + core * half, half), :]),
        (w_down, w_mix.at[cols(2 * width + core * down_half, down_half), :]),
    ]
    own_copies = []
    for i, (source, target) in enumerate(pieces):
        copy = pltpu.make_async_copy(source, target, own_sem.at[i])
        copy.start()
        own_copies.append(copy)

    barrier = pltpu.get_barrier_semaphore()
    for step in range(n - 1):
        pl.semaphore_signal(
            barrier, inc=1, device_id={"pa": owner(step)},
            device_id_type=pl.DeviceIdType.MESH,
        )
    pl.semaphore_signal(
        barrier, inc=1, device_id={"dev": sibling}, device_id_type=pl.DeviceIdType.MESH
    )

    table_copy.wait()

    def widen(i, carry):
        part = pl.ds(pl.multiple_of(i * 256, 256), 256)
        table_wide[part, :] = table_in[part, :].astype(F32)
        return carry

    lax.fori_loop(0, table_in.shape[0] // 256, widen, 0)
    blocks[...] = (
        lax.broadcasted_iota(jnp.int32, blocks.shape, 0) // history
        == lax.broadcasted_iota(jnp.int32, blocks.shape, 1) // head
    ).astype(F32).astype(BF16)
    for copy in feat_copies:
        copy.wait()
    pl.semaphore_wait(barrier, n)

    wcopies = []
    for i, (source, target) in enumerate(pieces):
        wcopies.append(
            pltpu.make_async_remote_copy(
                source, target, wsend_sem.at[i], wrecv_sem.at[i],
                device_id={"dev": sibling}, device_id_type=pl.DeviceIdType.MESH,
            )
        )

    def send_of(c, step):
        return pltpu.make_async_remote_copy(
            stage.at[step, pl.ds(c * chunk, chunk)],
            recv.at[pl.ds(c * chunk, chunk), pl.ds(pl.multiple_of(me * span, span), span), :],
            send_sem.at[c, step],
            recv_sem.at[c, step],
            device_id={"pa": owner(step)},
            device_id_type=pl.DeviceIdType.MESH,
        )

    def prepare(c, carry):
        for step in range(n):
            start = (first_user(step) + c * chunk) * span

            def fetch(i, inner):
                for p in range(span):
                    rows[pl.ds(i * span + p, 1), :] = table_wide[
                        pl.ds(ids[start + i * span + p], 1), :
                    ]
                return inner

            lax.fori_loop(0, chunk, fetch, 0)
            where = pl.ds(c * chunk, chunk)
            total = (
                stage[step, where].astype(F32) + rows[...].reshape(chunk, span, width)
            ).astype(BF16)
            if step < n - 1:
                stage[step, where] = total
            else:
                recv[where, pl.ds(pl.multiple_of(me * span, span), span), :] = total
            if step >= 1:
                send_of(c, step - 1).start()
        return carry

    prepare(0, 0)
    for copy in wcopies:
        copy.start()
    lax.fori_loop(1, chunks, prepare, 0)
    for copy in own_copies:
        copy.wait()
    for copy in wcopies:
        copy.wait()

    span_rows = GROUP * history
    ff = w_in.shape[1] - 3 * width
    lane = lax.broadcasted_iota(jnp.int32, (history, HEADS * history), 1)
    key_spot = lax.rem(lane, history)

    def lengths_of(g):
        length_at = (me * 2 + core) * share + g * GROUP
        return [lens[length_at + u] for u in range(GROUP)]

    def encode(g):
        lengths = lengths_of(g)
        x = recv[pl.ds(g * GROUP, GROUP)].reshape(span_rows, width)
        for f in range(0, 3 * width, width):
            qkv[:, f : f + width] = dot(x, w_in[:, f : f + width]).astype(BF16)
            yield
        ats = [pl.ds(u * history, history) for u in range(GROUP)]
        for u, at in enumerate(ats):
            keys = jnp.concatenate([qkv[at, width : 2 * width]] * HEADS, axis=0) * blocks[...]
            scores = lax.dot_general(
                qkv[at, :width], keys, NT, preferred_element_type=F32
            ) * (1.0 / head**0.5)
            probs = jnp.where(key_spot < lengths[u], jnp.exp(scores), 0.0)
            top = probs.astype(BF16)
            high[at, :] = top
            low[at, :] = (probs - top.astype(F32)).astype(BF16)
            if u % 2:
                yield
        for f in range(0, ff, 256):
            up = dot(x, w_in[:, 3 * width + f : 3 * width + f + 256])
            mix[:, width + f : width + f + 256] = jax.nn.gelu(up).astype(BF16)
            yield
        for u, at in enumerate(ats):
            values = jnp.concatenate([qkv[at, 2 * width :]] * HEADS, axis=0) * blocks[...]
            weighted[at, :] = dot(high[at, :], values)
            if u % 2:
                yield
        totals = dot(high[...], blocks[...]) + dot(low[...], blocks[...])
        mix[:, :width] = (weighted[...] / totals).astype(BF16)
        yield
        made = (dot(x, w_mix[:width, :]) + dot(mix[...], w_mix[width:, :])).astype(BF16)
        interests[lax.rem(g, 2)] = made

    def route(g):
        lengths = lengths_of(g)
        slot = lax.rem(g, 2)
        row = lax.broadcasted_iota(jnp.int32, (GROUP, span_rows), 0)
        col = lax.broadcasted_iota(jnp.int32, (GROUP, span_rows), 1)
        limit = jnp.zeros((GROUP, span_rows), jnp.int32)
        for u in range(GROUP):
            limit = jnp.where(row == u, u * history + lengths[u], limit)
        valid = ((col >= row * history) & (col < limit)).astype(F32)
        logits = [base[j * GROUP : (j + 1) * GROUP, :] for j in range(CAPS)]
        capsules = None
        for sweep in range(ITERS):
            peak = functools.reduce(jnp.maximum, logits)
            powers = [jnp.exp(l - peak) for l in logits]
            scale = valid / functools.reduce(jnp.add, powers)
            weights = jnp.concatenate([p * scale for p in powers], axis=0)
            both = dot(split(weights), interests[slot])
            yield
            yield
            summed = both[: CAPS * GROUP] + both[CAPS * GROUP :]
            squares = jnp.sum(summed * summed, axis=1, keepdims=True)
            yield
            capsules = summed * (jnp.sqrt(squares) / (1.0 + squares))
            if sweep + 1 < ITERS:
                both = lax.dot_general(
                    split(capsules), interests[slot], NT, preferred_element_type=F32
                )
                yield
                yield
                gain = both[: CAPS * GROUP] + both[CAPS * GROUP :]
                logits = [
                    l + gain[j * GROUP : (j + 1) * GROUP] for j, l in enumerate(logits)
                ]
        mine = jnp.where(core == 0, capsules[:, :half], capsules[:, half:])
        theirs = jnp.where(core == 0, capsules[:, half:], capsules[:, :half])
        first = g * GROUP * CAPS
        for j in range(CAPS):
            part = slice(j * GROUP, (j + 1) * GROUP)
            spot = pl.multiple_of(core * share * CAPS + first, GROUP * CAPS) + j
            out[pl.ds(spot, GROUP, stride=CAPS), :] = mine[part]
            spot = pl.multiple_of(first, GROUP * CAPS) + j
            outbox[pl.ds(spot, GROUP, stride=CAPS), :] = theirs[part]

    def interleave(*parts):
        parts = list(parts)
        while parts:
            for part in list(parts):
                try:
                    next(part)
                except StopIteration:
                    parts.remove(part)

    size = GROUP * CAPS

    def exchange(c):
        return pltpu.make_async_remote_copy(
            outbox.at[pl.ds(pl.multiple_of(c * size, size), size), :],
            out.at[pl.ds(pl.multiple_of(core * share * CAPS + c * size, size), size), :],
            xsend_sem.at[c],
            xrecv_sem.at[c],
            device_id={"dev": sibling},
            device_id_type=pl.DeviceIdType.MESH,
        )

    def arrive(c):
        for step in range(n - 1):
            send_of(c, step).wait_recv()

    arrive(0)
    interleave(encode(0))

    def consume(c, carry):
        arrive(c)
        interleave(route(c - 1), encode(c))

        @pl.when(c > 1)
        def _():
            exchange(c - 2).start()

        return carry

    lax.fori_loop(1, chunks, consume, 0)
    interleave(route(chunks - 1))
    for c in range(max(chunks - 2, 0), chunks):
        exchange(c).start()

    def drain(c, carry):
        exchange(c).wait()
        for step in range(n - 1):
            send_of(c, step).wait_send()
        return carry

    lax.fori_loop(0, chunks, drain, 0)


def body(
    features, item_ids, item_table, lengths, routing_seed, w_qkv, w_out, w_bilinear, w_up, w_down
):
    n = lax.axis_size("pa")
    cores = lax.axis_size("dev")
    span, width = features.shape[1:]
    owned = lengths.shape[0] // n
    share = owned // cores
    chunk = GROUP
    history = n * span
    if cores != 2 or span % 16 or share % chunk or n < 2 or history * HEADS != width:
        return plain_body(
            features, item_ids, item_table, lengths, routing_seed,
            w_qkv, w_out, w_bilinear, w_up, w_down,
        )
    chunks = share // chunk
    base = (routing_seed.astype(F32) - 7.5) * 0.25
    base = jnp.repeat(jnp.tile(base, (1, GROUP)), GROUP, axis=0)
    rows = GROUP * history
    ff = w_up.shape[1] * cores
    anywhere = pl.BlockSpec(memory_space=pl.ANY)
    vmem = pl.BlockSpec(memory_space=pltpu.VMEM)
    smem = pl.BlockSpec(memory_space=pltpu.SMEM)
    dma = pltpu.SemaphoreType.DMA
    routed = pl.pallas_call(
        functools.partial(fused, n, share, chunk),
        out_shape=jax.ShapeDtypeStruct((owned * CAPS, width // cores), F32),
        in_specs=[smem, smem, anywhere, anywhere, vmem] + [anywhere] * 5,
        out_specs=vmem,
        scratch_shapes=[
            pltpu.VMEM((n, share, span, width), BF16),
            pltpu.VMEM((share, history, width), BF16),
            pltpu.VMEM(item_table.shape, BF16),
            pltpu.VMEM(item_table.shape, F32),
            pltpu.VMEM((chunk * span, width), F32),
            pltpu.VMEM((width, 3 * width + ff), BF16),
            pltpu.VMEM((2 * width + ff, width), BF16),
            pltpu.VMEM((HEADS * history, width), BF16),
            pltpu.VMEM((rows, 3 * width), BF16),
            pltpu.VMEM((rows, width + ff), BF16),
            pltpu.VMEM((rows, width), BF16),
            pltpu.VMEM((rows, width), BF16),
            pltpu.VMEM((rows, width), F32),
            pltpu.VMEM((2, rows, width), BF16),
            pltpu.VMEM((share * CAPS, width // cores), F32),
            dma((n,)), dma, dma((7,)), dma((7,)), dma((7,)),
            dma((chunks, n - 1)), dma((chunks, n - 1)), dma((chunks,)), dma((chunks,)),
        ],
        compiler_params=pltpu.CompilerParams(
            collective_id=0, has_side_effects=True, vmem_limit_bytes=60 * 1024 * 1024
        ),
        name="encode_route",
    )(
        item_ids.reshape(-1), lengths, features, item_table, base,
        w_qkv, w_out, w_bilinear, w_up, w_down,
    )
    return routed.reshape(owned, CAPS, width // cores)


def solution(mesh):
    in_specs = (
        P("au", "pa", None),
        P("au", "pa"),
        P(),
        P("au"),
        P(),
        P(None, None, "dev"),
        P("dev", None),
        P(None, "dev"),
        P(None, "dev"),
        P("dev", None),
    )
    out_specs = P(("au", "pa"), None, "dev")
    return jax.shard_map(body, mesh=mesh, in_specs=in_specs, out_specs=out_specs, check_vma=False)
```

profile of v0, /device:TPU:0, one launch (start us, length us, event | category | flops | bytes accessed | tf_op | source)
XLA Modules:
  0.0 113.6 jit_solution(2367266793512707425)
XLA Ops:
  0.0 0.7 add_multiply_fusion
  0.7 0.1 tile.10
  0.8 0.6 broadcast_bitcast_fusion.base
  1.4 1.0 copy.11
  2.4 0.8 reshape.13.ids
  3.3 108.5 %encode_route.1 = f32[1024,128]{1,0:T(8,128)} custom-call(s32[16384]{0:T(1024)} %reshape.13.ids, s32[1024]{0:T(1024)} %lens.1, bf16[1024,16,256]{2,1,0:T(8,128)(2,1)} %feats.1, bf16[4096,256]{1,0:T(8,128)(2,1)} %table.1, f32[32,512]{1,0:T(8,128)} %broadcast_bitcast_fusion.base, bf16[3,256,128]{2,1,0:T(8,128)(2,1)} %w_qkv.1, bf16[128,256]{1,0:T(8,128)(2,1)} %w_out.1, ...), custom_call_target="tpu_custom_call" | custom-call | tf_op jit(solution)/shard_map/encode_route/pallas_call | solution.py:425
  111.7 1.9 %copy.13 = f32[256,4,128]{2,1,0:T(4,128)} copy(f32[256,4,128]{2,1,0:T(4,128)} %bitcast.3) | data formatting | bytes 1048576
  (1 shorter events, 0.0 us)
where the time goes:
time: 114 us
  Pallas kernels  108 us (95%)
  local copies, waits for them, and re-layouts  4.43 us (4%)
    pallas_call x1, Pallas kernels, body(): pl.pallas_call(functools.partial(fused, n, share, chunk), out_shape=jax.S...  108 us
    unnamed x2, local copies, waits for them, and re-layouts  2.9 us

commit v1 on v0

--- a/solution.py
+++ b/solution.py
@@ -120,6 +120,7 @@
 GROUP = 8
 F32, BF16 = jnp.float32, jnp.bfloat16
 NT = (((1,), (1,)), ((), ()))
+MESH = pl.DeviceIdType.MESH
 
 
 def dot(a, b):
@@ -132,11 +133,22 @@
     return jnp.concatenate([high, low], axis=0)
 
 
+def interleave(*parts):
+    parts = list(parts)
+    while parts:
+        for part in list(parts):
+            try:
+                next(part)
+            except StopIteration:
+                parts.remove(part)
+
+
 def fused(
-    n, share, chunk, ids, lens, feats, table, base, w_qkv, w_out, w_bil, w_up, w_down,
-    out, stage, recv, table_in, table_wide, rows, w_in, w_mix, blocks, qkv, mix, high, low,
-    weighted, interests, outbox, feat_sem, table_sem, own_sem, wsend_sem, wrecv_sem, send_sem, recv_sem,
-    xsend_sem, xrecv_sem,
+    n, share, ids, lens, feats, table, seed, w_qkv, w_out, w_bil, w_up, w_down,
+    out, recv, ids_vmem, ids_smem, table_in, table_wide, rows, x_ref, base, w_in, w_mix, blocks,
+    qkv, mix, high, low, weighted, interests, outbox,
+    table_sem, own_sem, id_sem, idsend_sem, idrecv_sem, wown_sem, wsend_sem, wrecv_sem,
+    send_sem, recv_sem, xsend_sem, xrecv_sem,
 ):
     me = lax.axis_index("pa")
     core = lax.axis_index("dev")
@@ -145,23 +157,34 @@
     history = n * span
     head = width // HEADS
     half = width // 2
-    chunks = share // chunk
+    chunks = share // GROUP
+    part = GROUP // 2
+    pieces = [(c * GROUP, GROUP) for c in range(chunks - 1)]
+    pieces += [(share - GROUP, part), (share - part, part)]
 
     def owner(step):
         return lax.rem(me + step + 1, n)
 
-    def first_user(step):
-        return (owner(step) * 2 + core) * share
+    def first_user(who):
+        return pl.multiple_of((who * 2 + core) * share, share)
+
+    barrier = pltpu.get_barrier_semaphore()
+    for step in range(n - 1):
+        pl.semaphore_signal(barrier, inc=1, device_id={"pa": owner(step)}, device_id_type=MESH)
+    pl.semaphore_signal(barrier, inc=1, device_id={"dev": sibling}, device_id_type=MESH)
 
     table_copy = pltpu.make_async_copy(table, table_in, table_sem)
     table_copy.start()
-    feat_copies = []
-    for step in range(n):
-        copy = pltpu.make_async_copy(
-            feats.at[pl.ds(first_user(step), share)], stage.at[step], feat_sem.at[step]
-        )
-        copy.start()
-        feat_copies.append(copy)
+    own_feats = pltpu.make_async_copy(
+        feats.at[pl.ds(first_user(me), share)],
+        recv.at[:, pl.ds(pl.multiple_of(me * span, span), span), :],
+        own_sem,
+    )
+    own_feats.start()
+    own_ids = pltpu.make_async_copy(
+        ids.at[:, pl.ds(first_user(me), share)], ids_vmem.at[me], id_sem.at[0]
+    )
+    own_ids.start()
 
     up_half = w_up.shape[1]
     down_half = w_down.shape[0]
@@ -169,7 +192,7 @@
     def cols(start, size):
         return pl.ds(pl.multiple_of(start, 128), size)
 
-    pieces = [
+    weights = [
         (w_qkv.at[i], w_in.at[:, cols(i * width + core * half, half)]) for i in range(3)
     ] + [
         (w_up, w_in.at[:, cols(3 * width + core * up_half, up_half)]),
@@ -178,91 +201,101 @@
         (w_down, w_mix.at[cols(2 * width + core * down_half, down_half), :]),
     ]
     own_copies = []
-    for i, (source, target) in enumerate(pieces):
-        copy = pltpu.make_async_copy(source, target, own_sem.at[i])
+    for i, (source, target) in enumerate(weights):
+        copy = pltpu.make_async_copy(source, target, wown_sem.at[i])
         copy.start()
         own_copies.append(copy)
 
-    barrier = pltpu.get_barrier_semaphore()
+    def send_ids(step):
+        return pltpu.make_async_remote_copy(
+            ids.at[:, pl.ds(first_user(owner(step)), share)],
+            ids_vmem.at[me],
+            idsend_sem.at[step],
+            idrecv_sem.at[step],
+            device_id={"pa": owner(step)},
+            device_id_type=MESH,
+        )
+
+    def send_of(p, start, size, step):
+        return pltpu.make_async_remote_copy(
+            feats.at[pl.ds(first_user(owner(step)) + start, size)],
+            recv.at[pl.ds(start, size), pl.ds(pl.multiple_of(me * span, span), span), :],
+            send_sem.at[p, step],
+            recv_sem.at[p, step],
+            device_id={"pa": owner(step)},
+            device_id_type=MESH,
+        )
+
+    wcopies = []
+    for i, (source, target) in enumerate(weights):
+        wcopies.append(
+            pltpu.make_async_remote_copy(
+                source, target, wsend_sem.at[i], wrecv_sem.at[i],
+                device_id={"dev": sibling}, device_id_type=MESH,
+            )
+        )
+
+    pl.semaphore_wait(barrier, n)
     for step in range(n - 1):
-        pl.semaphore_signal(
-            barrier, inc=1, device_id={"pa": owner(step)},
-            device_id_type=pl.DeviceIdType.MESH,
+        send_ids(step).start()
+
+    def launch(c, carry):
+        for step in range(n - 1):
+            send_of(c, c * GROUP, GROUP, step).start()
+        return carry
+
+    launch(0, 0)
+    for copy in wcopies:
+        copy.start()
+    lax.fori_loop(1, chunks - 1, launch, 0)
+    for p in (chunks - 1, chunks):
+        for step in range(n - 1):
+            send_of(p, *pieces[p], step).start()
+
+    base_here = (seed[...].astype(F32) - 7.5) * 0.25
+    base_here = jnp.concatenate([base_here] * GROUP, axis=1)
+    for j in range(CAPS):
+        base[j * GROUP : (j + 1) * GROUP, :] = jnp.broadcast_to(
+            base_here[j : j + 1], (GROUP, GROUP * history)
         )
-    pl.semaphore_signal(
-        barrier, inc=1, device_id={"dev": sibling}, device_id_type=pl.DeviceIdType.MESH
-    )
-
-    table_copy.wait()
-
-    def widen(i, carry):
-        part = pl.ds(pl.multiple_of(i * 256, 256), 256)
-        table_wide[part, :] = table_in[part, :].astype(F32)
-        return carry
-
-    lax.fori_loop(0, table_in.shape[0] // 256, widen, 0)
     blocks[...] = (
         lax.broadcasted_iota(jnp.int32, blocks.shape, 0) // history
         == lax.broadcasted_iota(jnp.int32, blocks.shape, 1) // head
     ).astype(F32).astype(BF16)
-    for copy in feat_copies:
-        copy.wait()
-    pl.semaphore_wait(barrier, n)
-
-    wcopies = []
-    for i, (source, target) in enumerate(pieces):
-        wcopies.append(
-            pltpu.make_async_remote_copy(
-                source, target, wsend_sem.at[i], wrecv_sem.at[i],
-                device_id={"dev": sibling}, device_id_type=pl.DeviceIdType.MESH,
-            )
-        )
-
-    def send_of(c, step):
-        return pltpu.make_async_remote_copy(
-            stage.at[step, pl.ds(c * chunk, chunk)],
-            recv.at[pl.ds(c * chunk, chunk), pl.ds(pl.multiple_of(me * span, span), span), :],
-            send_sem.at[c, step],
-            recv_sem.at[c, step],
-            device_id={"pa": owner(step)},
-            device_id_type=pl.DeviceIdType.MESH,
-        )
-
-    def prepare(c, carry):
-        for step in range(n):
-            start = (first_user(step) + c * chunk) * span
-
-            def fetch(i, inner):
+
+    table_copy.wait()
+
+    def widen(i, carry):
+        at = pl.ds(pl.multiple_of(i * 256, 256), 256)
+        for h in range(2):
+            table_wide[pl.ds(pl.multiple_of(i * 512, 512) + h, 256, stride=2), :] = table_in[
+                at, h * half : (h + 1) * half
+            ].astype(F32)
+        return carry
+
+    lax.fori_loop(0, table_in.shape[0] // 256, widen, 0)
+
+    own_ids.wait()
+    for step in range(n - 1):
+        send_ids(step).wait_recv()
+    id_copy = pltpu.make_async_copy(ids_vmem, ids_smem, id_sem.at[1])
+    id_copy.start()
+    id_copy.wait()
+
+    def gather(c):
+        def fetch(u, carry):
+            for z in range(n):
                 for p in range(span):
-                    rows[pl.ds(i * span + p, 1), :] = table_wide[
-                        pl.ds(ids[start + i * span + p], 1), :
+                    spot = pl.multiple_of(u * 2 * history, 2 * history) + 2 * (z * span + p)
+                    rows[pl.ds(spot, 2), :] = table_wide[
+                        pl.ds(ids_smem[z, p, c * GROUP + u] * 2, 2), :
                     ]
-                return inner
-
-            lax.fori_loop(0, chunk, fetch, 0)
-            where = pl.ds(c * chunk, chunk)
-            total = (
-                stage[step, where].astype(F32) + rows[...].reshape(chunk, span, width)
-            ).astype(BF16)
-            if step < n - 1:
-                stage[step, where] = total
-            else:
-                recv[where, pl.ds(pl.multiple_of(me * span, span), span), :] = total
-            if step >= 1:
-                send_of(c, step - 1).start()
-        return carry
-
-    prepare(0, 0)
-    for copy in wcopies:
-        copy.start()
-    lax.fori_loop(1, chunks, prepare, 0)
-    for copy in own_copies:
-        copy.wait()
-    for copy in wcopies:
-        copy.wait()
-
+            return carry
+
+        lax.fori_loop(0, GROUP, fetch, 0)
+
+    ff = w_in.shape[1] - 3 * width
     span_rows = GROUP * history
-    ff = w_in.shape[1] - 3 * width
     lane = lax.broadcasted_iota(jnp.int32, (history, HEADS * history), 1)
     key_spot = lax.rem(lane, history)
 
@@ -270,14 +303,23 @@
         length_at = (me * 2 + core) * share + g * GROUP
         return [lens[length_at + u] for u in range(GROUP)]
 
-    def encode(g):
+    def encode(g, first=0, users=GROUP):
         lengths = lengths_of(g)
-        x = recv[pl.ds(g * GROUP, GROUP)].reshape(span_rows, width)
+        span_here = slice(first * history, (first + users) * history)
+        count = users * history
+        feats_here = recv[pl.ds(g * GROUP + first, users)].reshape(count, width)
+        for h in range(2):
+            columns = slice(h * half, (h + 1) * half)
+            x_ref[span_here, columns] = (
+                feats_here[:, columns].astype(F32)
+                + rows[pl.ds(2 * first * history + h, count, stride=2), :]
+            ).astype(BF16)
+        x = x_ref[span_here, :]
         for f in range(0, 3 * width, width):
-            qkv[:, f : f + width] = dot(x, w_in[:, f : f + width]).astype(BF16)
+            qkv[span_here, f : f + width] = dot(x, w_in[:, f : f + width]).astype(BF16)
             yield
-        ats = [pl.ds(u * history, history) for u in range(GROUP)]
-        for u, at in enumerate(ats):
+        ats = [(u, pl.ds(u * history, history)) for u in range(first, first + users)]
+        for u, at in ats:
             keys = jnp.concatenate([qkv[at, width : 2 * width]] * HEADS, axis=0) * blocks[...]
             scores = lax.dot_general(
                 qkv[at, :width], keys, NT, preferred_element_type=F32
@@ -290,18 +332,18 @@
                 yield
         for f in range(0, ff, 256):
             up = dot(x, w_in[:, 3 * width + f : 3 * width + f + 256])
-            mix[:, width + f : width + f + 256] = jax.nn.gelu(up).astype(BF16)
+            mix[span_here, width + f : width + f + 256] = jax.nn.gelu(up).astype(BF16)
             yield
-        for u, at in enumerate(ats):
+        for u, at in ats:
             values = jnp.concatenate([qkv[at, 2 * width :]] * HEADS, axis=0) * blocks[...]
             weighted[at, :] = dot(high[at, :], values)
             if u % 2:
                 yield
-        totals = dot(high[...], blocks[...]) + dot(low[...], blocks[...])
-        mix[:, :width] = (weighted[...] / totals).astype(BF16)
+        totals = dot(high[span_here, :], blocks[...]) + dot(low[span_here, :], blocks[...])
+        mix[span_here, :width] = (weighted[span_here, :] / totals).astype(BF16)
         yield
-        made = (dot(x, w_mix[:width, :]) + dot(mix[...], w_mix[width:, :])).astype(BF16)
-        interests[lax.rem(g, 2)] = made
+        made = (dot(x, w_mix[:width, :]) + dot(mix[span_here, :], w_mix[width:, :])).astype(BF16)
+        interests[lax.rem(g, 2), span_here, :] = made
 
     def route(g):
         lengths = lengths_of(g)
@@ -318,8 +360,8 @@
             peak = functools.reduce(jnp.maximum, logits)
             powers = [jnp.exp(l - peak) for l in logits]
             scale = valid / functools.reduce(jnp.add, powers)
-            weights = jnp.concatenate([p * scale for p in powers], axis=0)
-            both = dot(split(weights), interests[slot])
+            weights_here = jnp.concatenate([p * scale for p in powers], axis=0)
+            both = dot(split(weights_here), interests[slot])
             yield
             yield
             summed = both[: CAPS * GROUP] + both[CAPS * GROUP :]
@@ -340,20 +382,11 @@
         theirs = jnp.where(core == 0, capsules[:, half:], capsules[:, :half])
         first = g * GROUP * CAPS
         for j in range(CAPS):
-            part = slice(j * GROUP, (j + 1) * GROUP)
+            here = slice(j * GROUP, (j + 1) * GROUP)
             spot = pl.multiple_of(core * share * CAPS + first, GROUP * CAPS) + j
-            out[pl.ds(spot, GROUP, stride=CAPS), :] = mine[part]
+            out[pl.ds(spot, GROUP, stride=CAPS), :] = mine[here]
             spot = pl.multiple_of(first, GROUP * CAPS) + j
-            outbox[pl.ds(spot, GROUP, stride=CAPS), :] = theirs[part]
-
-    def interleave(*parts):
-        parts = list(parts)
-        while parts:
-            for part in list(parts):
-                try:
-                    next(part)
-                except StopIteration:
-                    parts.remove(part)
+            outbox[pl.ds(spot, GROUP, stride=CAPS), :] = theirs[here]
 
     size = GROUP * CAPS
 
@@ -364,19 +397,28 @@
             xsend_sem.at[c],
             xrecv_sem.at[c],
             device_id={"dev": sibling},
-            device_id_type=pl.DeviceIdType.MESH,
+            device_id_type=MESH,
         )
 
-    def arrive(c):
+    def arrive(p, start, size):
         for step in range(n - 1):
-            send_of(c, step).wait_recv()
-
-    arrive(0)
+            send_of(p, start, size, step).wait_recv()
+
+    gather(0)
+    own_feats.wait()
+    for copy in own_copies:
+        copy.wait()
+    for copy in wcopies:
+        copy.wait()
+
+    arrive(0, 0, GROUP)
     interleave(encode(0))
+    gather(1)
 
     def consume(c, carry):
-        arrive(c)
+        arrive(c, c * GROUP, GROUP)
         interleave(route(c - 1), encode(c))
+        gather(c + 1)
 
         @pl.when(c > 1)
         def _():
@@ -384,18 +426,30 @@
 
         return carry
 
-    lax.fori_loop(1, chunks, consume, 0)
-    interleave(route(chunks - 1))
-    for c in range(max(chunks - 2, 0), chunks):
-        exchange(c).start()
+    last = chunks - 1
+    lax.fori_loop(1, last, consume, 0)
+    interleave(route(last - 1))
+    exchange(last - 2).start()
+    arrive(last, *pieces[last])
+    interleave(encode(last, 0, part))
+    exchange(last - 1).start()
+    arrive(chunks, *pieces[chunks])
+    interleave(encode(last, part, part))
+    interleave(route(last))
+    exchange(last).start()
 
     def drain(c, carry):
         exchange(c).wait()
         for step in range(n - 1):
-            send_of(c, step).wait_send()
+            send_of(c, c * GROUP, GROUP, step).wait_send()
         return carry
 
-    lax.fori_loop(0, chunks, drain, 0)
+    for step in range(n - 1):
+        send_ids(step).wait_send()
+        for p in (chunks - 1, chunks):
+            send_of(p, *pieces[p], step).wait_send()
+    lax.fori_loop(0, last, drain, 0)
+    exchange(last).wait()
 
 
 def body(
@@ -406,33 +460,36 @@
     span, width = features.shape[1:]
     owned = lengths.shape[0] // n
     share = owned // cores
-    chunk = GROUP
     history = n * span
-    if cores != 2 or span % 16 or share % chunk or n < 2 or history * HEADS != width:
+    if (
+        cores != 2 or span % 16 or share % 128 or n < 2 or history * HEADS != width
+        or item_table.shape[0] % 256
+    ):
         return plain_body(
             features, item_ids, item_table, lengths, routing_seed,
             w_qkv, w_out, w_bilinear, w_up, w_down,
         )
-    chunks = share // chunk
-    base = (routing_seed.astype(F32) - 7.5) * 0.25
-    base = jnp.repeat(jnp.tile(base, (1, GROUP)), GROUP, axis=0)
+    chunks = share // GROUP
     rows = GROUP * history
     ff = w_up.shape[1] * cores
-    anywhere = pl.BlockSpec(memory_space=pl.ANY)
+    hbm = pl.BlockSpec(memory_space=pltpu.HBM)
     vmem = pl.BlockSpec(memory_space=pltpu.VMEM)
     smem = pl.BlockSpec(memory_space=pltpu.SMEM)
     dma = pltpu.SemaphoreType.DMA
     routed = pl.pallas_call(
-        functools.partial(fused, n, share, chunk),
+        functools.partial(fused, n, share),
         out_shape=jax.ShapeDtypeStruct((owned * CAPS, width // cores), F32),
-        in_specs=[smem, smem, anywhere, anywhere, vmem] + [anywhere] * 5,
+        in_specs=[hbm, smem, hbm, hbm, vmem] + [hbm] * 5,
         out_specs=vmem,
         scratch_shapes=[
-            pltpu.VMEM((n, share, span, width), BF16),
             pltpu.VMEM((share, history, width), BF16),
+            pltpu.VMEM((n, span, share), jnp.int32),
+            pltpu.SMEM((n, span, share), jnp.int32),
             pltpu.VMEM(item_table.shape, BF16),
-            pltpu.VMEM(item_table.shape, F32),
-            pltpu.VMEM((chunk * span, width), F32),
+            pltpu.VMEM((item_table.shape[0] * 2, width // 2), F32),
+            pltpu.VMEM((rows * 2, width // 2), F32),
+            pltpu.VMEM((rows, width), BF16),
+            pltpu.VMEM((CAPS * GROUP, rows), F32),
             pltpu.VMEM((width, 3 * width + ff), BF16),
             pltpu.VMEM((2 * width + ff, width), BF16),
             pltpu.VMEM((HEADS * history, width), BF16),
@@ -443,18 +500,21 @@
             pltpu.VMEM((rows, width), F32),
             pltpu.VMEM((2, rows, width), BF16),
             pltpu.VMEM((share * CAPS, width // cores), F32),
-            dma((n,)), dma, dma((7,)), dma((7,)), dma((7,)),
-            dma((chunks, n - 1)), dma((chunks, n - 1)), dma((chunks,)), dma((chunks,)),
+            dma, dma, dma((2,)), dma((n - 1,)), dma((n - 1,)), dma((7,)), dma((7,)), dma((7,)),
+            dma((chunks + 1, n - 1)), dma((chunks + 1, n - 1)), dma((chunks,)), dma((chunks,)),
         ],
         compiler_params=pltpu.CompilerParams(
-            collective_id=0, has_side_effects=True, vmem_limit_bytes=60 * 1024 * 1024
+            collective_id=0, has_side_effects=True, vmem_limit_bytes=VMEM_LIMIT
         ),
         name="encode_route",
     )(
-        item_ids.reshape(-1), lengths, features, item_table, base,
+        item_ids.T, lengths, features, item_table, routing_seed,
         w_qkv, w_out, w_bilinear, w_up, w_down,
     )
     return routed.reshape(owned, CAPS, width // cores)
+
+
+VMEM_LIMIT = 60 * 1024 * 1024
 
 
 def solution(mesh):

time: 114 us -> 114 us (level)
  Pallas kernels: 108 us -> 111 us
  local copies, waits for them, and re-layouts: 4.43 us -> 1.87 us
    pallas_call x1, Pallas kernels: 108 us -> 111 us  [body(): pl.pallas_call(functools.partial(fused, n, share), out_shape=jax.ShapeDty...]
    reshape x2 -> x0, local copies, waits for them, and re-layouts: 1.45 us -> none  [the longest x1 0.82 us: body(): item_ids.reshape(-1)]
    unnamed x2 -> x1, local copies, waits for them, and re-layouts: 2.9 us -> 1.87 us
where the time goes in v1:
time: 114 us; the launch traced here: 113 us
  Pallas kernels  111 us (97%)
  local copies, waits for them, and re-layouts  1.87 us (2%)
    pallas_call x1, Pallas kernels, body(): pl.pallas_call(functools.partial(fused, n, share), out_shape=jax.ShapeDty...  111 us

profile of v1, /device:TPU:0, one launch (start us, length us, event | category | flops | bytes accessed | tf_op | source)
XLA Modules:
  0.0 113.3 jit_solution(16106570202322297179)
XLA Ops:
  0.0 111.4 %encode_route.1 = f32[1024,128]{1,0:T(8,128)} custom-call(s32[16,1024]{1,0:T(8,128)} %bitcast.3, s32[1024]{0:T(1024)} %lens.1, bf16[1024,16,256]{2,1,0:T(8,128)(2,1)} %feats.1, bf16[4096,256]{1,0:T(8,128)(2,1)} %table.1, s32[4,64]{1,0:T(4,128)} %seed.1, bf16[3,256,128]{2,1,0:T(8,128)(2,1)} %w_qkv.1, bf16[128,256]{1,0:T(8,128)(2,1)} %w_out.1, ...), custom_call_target="tpu_custom_call" | custom-call | tf_op jit(solution)/shard_map/encode_route/pallas_call | solution.py:479
  111.4 1.9 %copy.12 = f32[256,4,128]{2,1,0:T(4,128)} copy(f32[256,4,128]{2,1,0:T(4,128)} %bitcast.2) | data formatting | bytes 1048576

commit v2 on v1

--- a/solution.py
+++ b/solution.py
@@ -144,10 +144,10 @@
 
 
 def fused(
-    n, share, ids, lens, feats, table, seed, w_qkv, w_out, w_bil, w_up, w_down,
-    out, recv, ids_vmem, ids_smem, table_in, table_wide, rows, x_ref, base, w_in, w_mix, blocks,
+    n, share, ids, lens_in, feats, table, seed_in, w_qkv, w_out, w_bil, w_up, w_down,
+    out, stage, recv, lens, seed, ids_vmem, ids_smem, table_in, table_wide, rows, x_ref, base, w_in, w_mix, blocks,
     qkv, mix, high, low, weighted, interests, outbox,
-    table_sem, own_sem, id_sem, idsend_sem, idrecv_sem, wown_sem, wsend_sem, wrecv_sem,
+    table_sem, own_sem, feat_sem, small_sem, id_sem, idsend_sem, idrecv_sem, wown_sem, wsend_sem, wrecv_sem,
     send_sem, recv_sem, xsend_sem, xrecv_sem,
 ):
     me = lax.axis_index("pa")
@@ -173,8 +173,21 @@
         pl.semaphore_signal(barrier, inc=1, device_id={"pa": owner(step)}, device_id_type=MESH)
     pl.semaphore_signal(barrier, inc=1, device_id={"dev": sibling}, device_id_type=MESH)
 
+    feat_copies = []
+    for step in range(n - 1):
+        copy = pltpu.make_async_copy(
+            feats.at[pl.ds(first_user(owner(step)), share)], stage.at[step], feat_sem.at[step]
+        )
+        copy.start()
+        feat_copies.append(copy)
     table_copy = pltpu.make_async_copy(table, table_in, table_sem)
     table_copy.start()
+    small_copies = [
+        pltpu.make_async_copy(lens_in, lens, small_sem.at[0]),
+        pltpu.make_async_copy(seed_in, seed, small_sem.at[1]),
+    ]
+    for copy in small_copies:
+        copy.start()
     own_feats = pltpu.make_async_copy(
         feats.at[pl.ds(first_user(me), share)],
         recv.at[:, pl.ds(pl.multiple_of(me * span, span), span), :],
@@ -218,7 +231,7 @@
 
     def send_of(p, start, size, step):
         return pltpu.make_async_remote_copy(
-            feats.at[pl.ds(first_user(owner(step)) + start, size)],
+            stage.at[step, pl.ds(start, size)],
             recv.at[pl.ds(start, size), pl.ds(pl.multiple_of(me * span, span), span), :],
             send_sem.at[p, step],
             recv_sem.at[p, step],
@@ -235,6 +248,8 @@
             )
         )
 
+    for copy in feat_copies:
+        copy.wait()
     pl.semaphore_wait(barrier, n)
     for step in range(n - 1):
         send_ids(step).start()
@@ -247,11 +262,10 @@
     launch(0, 0)
     for copy in wcopies:
         copy.start()
-    lax.fori_loop(1, chunks - 1, launch, 0)
-    for p in (chunks - 1, chunks):
-        for step in range(n - 1):
-            send_of(p, *pieces[p], step).start()
-
+    lax.fori_loop(1, AHEAD, launch, 0)
+
+    for copy in small_copies:
+        copy.wait()
     base_here = (seed[...].astype(F32) - 7.5) * 0.25
     base_here = jnp.concatenate([base_here] * GROUP, axis=1)
     for j in range(CAPS):
@@ -411,12 +425,25 @@
     for copy in wcopies:
         copy.wait()
 
+    def advance(c):
+        @pl.when(c + AHEAD < chunks - 1)
+        def _():
+            launch(c + AHEAD, 0)
+
+        @pl.when(c + AHEAD == chunks - 1)
+        def _():
+            for p in (chunks - 1, chunks):
+                for step in range(n - 1):
+                    send_of(p, *pieces[p], step).start()
+
     arrive(0, 0, GROUP)
+    advance(0)
     interleave(encode(0))
     gather(1)
 
     def consume(c, carry):
         arrive(c, c * GROUP, GROUP)
+        advance(c)
         interleave(route(c - 1), encode(c))
         gather(c + 1)
 
@@ -474,15 +501,17 @@
     ff = w_up.shape[1] * cores
     hbm = pl.BlockSpec(memory_space=pltpu.HBM)
     vmem = pl.BlockSpec(memory_space=pltpu.VMEM)
-    smem = pl.BlockSpec(memory_space=pltpu.SMEM)
     dma = pltpu.SemaphoreType.DMA
     routed = pl.pallas_call(
         functools.partial(fused, n, share),
         out_shape=jax.ShapeDtypeStruct((owned * CAPS, width // cores), F32),
-        in_specs=[hbm, smem, hbm, hbm, vmem] + [hbm] * 5,
+        in_specs=[hbm] * 10,
         out_specs=vmem,
         scratch_shapes=[
+            pltpu.VMEM((n - 1, share, span, width), BF16),
             pltpu.VMEM((share, history, width), BF16),
+            pltpu.SMEM(lengths.shape, jnp.int32),
+            pltpu.VMEM(routing_seed.shape, jnp.int32),
             pltpu.VMEM((n, span, share), jnp.int32),
             pltpu.SMEM((n, span, share), jnp.int32),
             pltpu.VMEM(item_table.shape, BF16),
@@ -500,21 +529,22 @@
             pltpu.VMEM((rows, width), F32),
             pltpu.VMEM((2, rows, width), BF16),
             pltpu.VMEM((share * CAPS, width // cores), F32),
-            dma, dma, dma((2,)), dma((n - 1,)), dma((n - 1,)), dma((7,)), dma((7,)), dma((7,)),
+            dma, dma, dma((n - 1,)), dma((2,)), dma((2,)), dma((n - 1,)), dma((n - 1,)), dma((7,)), dma((7,)), dma((7,)),
             dma((chunks + 1, n - 1)), dma((chunks + 1, n - 1)), dma((chunks,)), dma((chunks,)),
         ],
         compiler_params=pltpu.CompilerParams(
             collective_id=0, has_side_effects=True, vmem_limit_bytes=VMEM_LIMIT
         ),
         name="encode_route",
-    )(
+    )(*(pltpu.with_memory_space_constraint(a, pltpu.HBM) for a in (
         item_ids.T, lengths, features, item_table, routing_seed,
         w_qkv, w_out, w_bilinear, w_up, w_down,
-    )
+    )))
     return routed.reshape(owned, CAPS, width // cores)
 
 
-VMEM_LIMIT = 60 * 1024 * 1024
+AHEAD = 2
+VMEM_LIMIT = 50 * 1024 * 1024
 
 
 def solution(mesh):

time: 114 us -> 105 us (0.921)
  Pallas kernels: 111 us -> 103 us
    pallas_call x1, Pallas kernels: 111 us -> 103 us  [body(): pl.pallas_call(functools.partial(fused, n, share), out_shape=jax.ShapeDty...]
where the time goes in v2:
time: 105 us; the launch traced here: 104 us
  Pallas kernels  103 us (98%)
    pallas_call x1, Pallas kernels, body(): pl.pallas_call(functools.partial(fused, n, share), out_shape=jax.ShapeDty...  103 us

profile of v2, /device:TPU:0, one launch (start us, length us, event | category | flops | bytes accessed | tf_op | source)
XLA Modules:
  0.0 104.0 jit_solution(11053797138748133961)
XLA Ops:
  0.0 103.2 %encode_route.1 = f32[1024,128]{1,0:T(8,128)S(1)} custom-call(s32[16,1024]{1,0:T(8,128)} %bitcast.3, s32[1024]{0:T(1024)} %lens_in.1, bf16[1024,16,256]{2,1,0:T(8,128)(2,1)} %feats.1, bf16[4096,256]{1,0:T(8,128)(2,1)} %table.1, s32[4,64]{1,0:T(4,128)} %seed_in.1, bf16[3,256,128]{2,1,0:T(8,128)(2,1)} %w_qkv.1, bf16[128,256]{1,0:T(8,128)(2,1)} %w_out.1, ...), custom_call_target="tpu_custom_call" | custom-call | tf_op jit(solution)/shard_map/encode_route/pallas_call | solution.py:505
  103.2 0.8 copy.12

commit v3 on v2

--- a/solution.py
+++ b/solution.py
@@ -254,6 +254,9 @@
     for step in range(n - 1):
         send_ids(step).start()
 
+    at_end = (me == 0) | (me == n - 1)
+    lead = jnp.where(at_end, AHEAD_END, AHEAD)
+
     def launch(c, carry):
         for step in range(n - 1):
             send_of(c, c * GROUP, GROUP, step).start()
@@ -262,7 +265,7 @@
     launch(0, 0)
     for copy in wcopies:
         copy.start()
-    lax.fori_loop(1, AHEAD, launch, 0)
+    lax.fori_loop(1, lead, launch, 0)
 
     for copy in small_copies:
         copy.wait()
@@ -296,11 +299,16 @@
     id_copy.start()
     id_copy.wait()
 
+    def slot_of(c):
+        return pl.multiple_of(lax.rem(c, 2) * 2 * GROUP * history, 2 * GROUP * history)
+
     def gather(c):
+        held = slot_of(c)
+
         def fetch(u, carry):
             for z in range(n):
                 for p in range(span):
-                    spot = pl.multiple_of(u * 2 * history, 2 * history) + 2 * (z * span + p)
+                    spot = held + pl.multiple_of(u * 2 * history, 2 * history) + 2 * (z * span + p)
                     rows[pl.ds(spot, 2), :] = table_wide[
                         pl.ds(ids_smem[z, p, c * GROUP + u] * 2, 2), :
                     ]
@@ -326,7 +334,7 @@
             columns = slice(h * half, (h + 1) * half)
             x_ref[span_here, columns] = (
                 feats_here[:, columns].astype(F32)
-                + rows[pl.ds(2 * first * history + h, count, stride=2), :]
+                + rows[pl.ds(slot_of(g) + 2 * first * history + h, count, stride=2), :]
             ).astype(BF16)
         x = x_ref[span_here, :]
         for f in range(0, 3 * width, width):
@@ -426,26 +434,26 @@
         copy.wait()
 
     def advance(c):
-        @pl.when(c + AHEAD < chunks - 1)
+        @pl.when(c + lead < chunks - 1)
         def _():
-            launch(c + AHEAD, 0)
-
-        @pl.when(c + AHEAD == chunks - 1)
+            launch(c + lead, 0)
+
+        @pl.when(c + lead == chunks - 1)
         def _():
             for p in (chunks - 1, chunks):
                 for step in range(n - 1):
                     send_of(p, *pieces[p], step).start()
 
+    gather(1)
     arrive(0, 0, GROUP)
     advance(0)
     interleave(encode(0))
-    gather(1)
 
     def consume(c, carry):
+        gather(c + 1)
         arrive(c, c * GROUP, GROUP)
         advance(c)
         interleave(route(c - 1), encode(c))
-        gather(c + 1)
 
         @pl.when(c > 1)
         def _():
@@ -454,14 +462,18 @@
         return carry
 
     last = chunks - 1
-    lax.fori_loop(1, last, consume, 0)
-    interleave(route(last - 1))
+    lax.fori_loop(1, last - 1, consume, 0)
+    exchange(last - 3).start()
+    gather(last)
+    interleave(route(last - 2))
+    arrive(last - 1, (last - 1) * GROUP, GROUP)
+    interleave(encode(last - 1))
     exchange(last - 2).start()
     arrive(last, *pieces[last])
     interleave(encode(last, 0, part))
+    arrive(chunks, *pieces[chunks])
+    interleave(route(last - 1), encode(last, part, part))
     exchange(last - 1).start()
-    arrive(chunks, *pieces[chunks])
-    interleave(encode(last, part, part))
     interleave(route(last))
     exchange(last).start()
 
@@ -489,7 +501,7 @@
     share = owned // cores
     history = n * span
     if (
-        cores != 2 or span % 16 or share % 128 or n < 2 or history * HEADS != width
+        cores != 2 or span % 16 or share % 128 or n < 2 or share < 4 * GROUP or history * HEADS != width
         or item_table.shape[0] % 256
     ):
         return plain_body(
@@ -516,7 +528,7 @@
             pltpu.SMEM((n, span, share), jnp.int32),
             pltpu.VMEM(item_table.shape, BF16),
             pltpu.VMEM((item_table.shape[0] * 2, width // 2), F32),
-            pltpu.VMEM((rows * 2, width // 2), F32),
+            pltpu.VMEM((2 * rows * 2, width // 2), F32),
             pltpu.VMEM((rows, width), BF16),
             pltpu.VMEM((CAPS * GROUP, rows), F32),
             pltpu.VMEM((width, 3 * width + ff), BF16),
@@ -543,7 +555,8 @@
     return routed.reshape(owned, CAPS, width // cores)
 
 
-AHEAD = 2
+AHEAD = 5
+AHEAD_END = 2
 VMEM_LIMIT = 50 * 1024 * 1024
 
 

time: 105 us -> 104 us (level)
  no operation moved by 1% of the time
where the time goes in v3:
time: 104 us
  Pallas kernels  103 us (99%)
    pallas_call x1, Pallas kernels, body(): pl.pallas_call(functools.partial(fused, n, share), out_shape=jax.ShapeDty...  103 us

profile of v3, /device:TPU:0, one launch (start us, length us, event | category | flops | bytes accessed | tf_op | source)
XLA Modules:
  0.0 103.5 jit_solution(14761510022599910812)
XLA Ops:
  0.0 102.7 %encode_route.1 = f32[1024,128]{1,0:T(8,128)S(1)} custom-call(s32[16,1024]{1,0:T(8,128)} %bitcast.3, s32[1024]{0:T(1024)} %lens_in.1, bf16[1024,16,256]{2,1,0:T(8,128)(2,1)} %feats.1, bf16[4096,256]{1,0:T(8,128)(2,1)} %table.1, s32[4,64]{1,0:T(4,128)} %seed_in.1, bf16[3,256,128]{2,1,0:T(8,128)(2,1)} %w_qkv.1, bf16[128,256]{1,0:T(8,128)(2,1)} %w_out.1, ...), custom_call_target="tpu_custom_call" | custom-call | tf_op jit(solution)/shard_map/encode_route/pallas_call | solution.py:517
  102.8 0.8 copy.12

commit v4 on v3

--- a/solution.py
+++ b/solution.py
@@ -158,9 +158,6 @@
     head = width // HEADS
     half = width // 2
     chunks = share // GROUP
-    part = GROUP // 2
-    pieces = [(c * GROUP, GROUP) for c in range(chunks - 1)]
-    pieces += [(share - GROUP, part), (share - part, part)]
 
     def owner(step):
         return lax.rem(me + step + 1, n)
@@ -434,15 +431,9 @@
         copy.wait()
 
     def advance(c):
-        @pl.when(c + lead < chunks - 1)
+        @pl.when(c + lead < chunks)
         def _():
             launch(c + lead, 0)
-
-        @pl.when(c + lead == chunks - 1)
-        def _():
-            for p in (chunks - 1, chunks):
-                for step in range(n - 1):
-                    send_of(p, *pieces[p], step).start()
 
     gather(1)
     arrive(0, 0, GROUP)
@@ -469,10 +460,8 @@
     arrive(last - 1, (last - 1) * GROUP, GROUP)
     interleave(encode(last - 1))
     exchange(last - 2).start()
-    arrive(last, *pieces[last])
-    interleave(encode(last, 0, part))
-    arrive(chunks, *pieces[chunks])
-    interleave(route(last - 1), encode(last, part, part))
+    arrive(last, last * GROUP, GROUP)
+    interleave(route(last - 1), encode(last))
     exchange(last - 1).start()
     interleave(route(last))
     exchange(last).start()
@@ -485,10 +474,7 @@
 
     for step in range(n - 1):
         send_ids(step).wait_send()
-        for p in (chunks - 1, chunks):
-            send_of(p, *pieces[p], step).wait_send()
-    lax.fori_loop(0, last, drain, 0)
-    exchange(last).wait()
+    lax.fori_loop(0, chunks, drain, 0)
 
 
 def body(
@@ -542,7 +528,7 @@
             pltpu.VMEM((2, rows, width), BF16),
             pltpu.VMEM((share * CAPS, width // cores), F32),
             dma, dma, dma((n - 1,)), dma((2,)), dma((2,)), dma((n - 1,)), dma((n - 1,)), dma((7,)), dma((7,)), dma((7,)),
-            dma((chunks + 1, n - 1)), dma((chunks + 1, n - 1)), dma((chunks,)), dma((chunks,)),
+            dma((chunks, n - 1)), dma((chunks, n - 1)), dma((chunks,)), dma((chunks,)),
         ],
         compiler_params=pltpu.CompilerParams(
             collective_id=0, has_side_effects=True, vmem_limit_bytes=VMEM_LIMIT
@@ -555,7 +541,7 @@
     return routed.reshape(owned, CAPS, width // cores)
 
 
-AHEAD = 5
+AHEAD = 3
 AHEAD_END = 2
 VMEM_LIMIT = 50 * 1024 * 1024
 

time: 104 us -> 104 us (level)
  no operation moved by 1% of the time
where the time goes in v4:
time: 104 us
  Pallas kernels  103 us (99%)
    pallas_call x1, Pallas kernels, body(): pl.pallas_call(functools.partial(fused, n, share), out_shape=jax.ShapeDty...  103 us

profile of v4, /device:TPU:0, one launch (start us, length us, event | category | flops | bytes accessed | tf_op | source)
XLA Modules:
  0.0 104.1 jit_solution(12513811719264405821)
XLA Ops:
  0.0 103.3 %encode_route.1 = f32[1024,128]{1,0:T(8,128)S(1)} custom-call(s32[16,1024]{1,0:T(8,128)} %bitcast.3, s32[1024]{0:T(1024)} %lens_in.1, bf16[1024,16,256]{2,1,0:T(8,128)(2,1)} %feats.1, bf16[4096,256]{1,0:T(8,128)(2,1)} %table.1, s32[4,64]{1,0:T(4,128)} %seed_in.1, bf16[3,256,128]{2,1,0:T(8,128)(2,1)} %w_qkv.1, bf16[128,256]{1,0:T(8,128)(2,1)} %w_out.1, ...), custom_call_target="tpu_custom_call" | custom-call | tf_op jit(solution)/shard_map/encode_route/pallas_call | solution.py:503
  103.3 0.8 copy.12
